TPU v7x, 32 devices: a whole 2x2x4 slice. The times are simulated.
32 devices in a mesh: groups: 2 (over x), col: 16 (over z, y, core).
Axes of the slice: x: 2, y: 2, z: 4, core: 2. Of those that a mesh axis runs over, the one named last changes fastest.
Arguments:
- left: bfloat16 [256, 64, 32], P('col', 'groups'), parts along dimension 1, may hold values from -18 to 18
- right: bfloat16 [256, 2560, 32], P('col', 'groups'), parts along dimension 1, may hold values from -18 to 18
- out_weight: bfloat16 [1024, 128], replicated, may hold values from -0.1875 to 0.1875
- out_bias: float32 [128], replicated, may hold values from -3 to 3
Outputs:
- pair_update: bfloat16 [64, 1280, 128], P('groups', 'col'), parts along dimension 0
There are 2 independent parts, one for each index of `groups`. A program takes and returns all parts, laid end to end along the dimension named above; an argument that names none is the same for every part. Nothing has to cross between parts.
All inputs are finite; a program needn't handle non-finite values.
Results may differ from a plain program's by a relative error of at most 0.004.
Values may be sent and summed in bfloat16 or wider, within the bound.
A program may use at most 64 MiB of HBM per device.

v0:
```python
import jax
import jax.numpy as jnp
from jax import lax
from jax.sharding import PartitionSpec as P


def tile_update(left_rows, right_cols, out_weight, out_bias):
    seqs, count, width = left_rows.shape
    columns = right_cols.shape[1]
    outer = (
        jnp.einsum("sic,sje->ijce", left_rows, right_cols, preferred_element_type=jnp.float32)
        / seqs
    )
    flat = outer.astype(jnp.bfloat16).reshape(count * columns, width * width)
    update = jnp.dot(flat, out_weight, preferred_element_type=jnp.float32) + out_bias
    return update.astype(jnp.bfloat16).reshape(count, columns, out_weight.shape[1])


def rows_update(left_rows, right_cols, out_weight, out_bias):
    seqs, count, width = left_rows.shape
    blocks = jnp.transpose(left_rows.reshape(seqs, count // 8, 8, width), (1, 0, 2, 3))
    results = lax.map(lambda block: tile_update(block, right_cols, out_weight, out_bias), blocks)
    return results.reshape(count, right_cols.shape[1], out_weight.shape[1])


def on_device(left, right, out_weight, out_bias):
    left_part, right_cols = (
        lax.all_to_all(left, "col", split_axis=1, concat_axis=0, tiled=True),
        lax.all_to_all(right, "col", split_axis=1, concat_axis=0, tiled=True),
    )
    return rows_update(
        lax.all_gather(left_part, "col", axis=1, tiled=True), right_cols, out_weight, out_bias
    )


def solution(mesh):
    in_specs = (P("col", "groups", None), P("col", "groups", None), P(), P())
    out_specs = P("groups", "col", None)
    return jax.shard_map(
        on_device, mesh=mesh, in_specs=in_specs, out_specs=out_specs, check_vma=False
    )
```

profile of v0, /device:TPU:9, one launch (start us, length us, event | category | flops | bytes accessed | tf_op | source)
XLA Modules:
  0.0 118.3 jit_solution(4670310625103489706)
XLA Ops:
  0.0 1.0 copy.21
  1.0 0.8 reshape.16
  1.7 6.6 %all-to-all-start = ((bf16[16,2,512]{2,1,0:T(2,128)(2,1)}), bf16[16,2,512]{2,1,0:T(2,128)(2,1)S(1)}, u32[]{:S(2)}, u32[]{:S(2)}) async-start(bf16[16,2,512]{2,1,0:T(2,128)(2,1)} %reshape.16), calls=%async_computation | async-start | bytes 65536 | tf_op jit(solution)/shard_map/all_to_all | solution.py:28
  8.3 6.9 %copy.16 = bf16[16,1280,32]{2,0,1:T(8,128)(2,1)} copy(bf16[16,1280,32]{1,2,0:T(8,128)(2,1)} %param.7) | data formatting | bytes 2621440 | tf_op args[1]
  15.2 8.3 %reshape.18 = bf16[16,2,20480]{2,1,0:T(2,128)(2,1)} reshape(bf16[1280,16,32]{2,1,0:T(8,128)(2,1)} %bitcast.49) | data formatting | bytes 2621440
  23.5 6.0 %all-to-all-start.1 = ((bf16[16,2,20480]{2,1,0:T(2,128)(2,1)}), bf16[16,2,20480]{2,1,0:T(2,128)(2,1)S(1)}, u32[]{:S(2)}, u32[]{:S(2)}) async-start(bf16[16,2,20480]{2,1,0:T(2,128)(2,1)} %reshape.18), calls=%async_computation.1 | async-start | bytes 2621440 | tf_op jit(solution)/shard_map/all_to_all | solution.py:29
  29.8 43.8 %all_gather.3 = bf16[256,32,32]{0,2,1:T(8,128)(2,1)} all-gather(bf16[256,2,32]{0,2,1:T(8,128)(2,1)S(1)} %copy.15), channel_id=1, replica_groups=mesh['groups'=2,'col'=16] {'col'}, dimensions={1}, use_global_device_ids=true | all-gather | bytes 557056 | tf_op jit(solution)/shard_map/all_gather | solution.py:32
  73.6 4.0 %reshape.19 = bf16[1280,16,32]{2,1,0:T(8,128)(2,1)} reshape(bf16[16,2,20480]{2,1,0:T(2,128)(2,1)S(1)} %all-to-all-done.1) | data formatting | bytes 2621440
  77.6 6.8 %copy.17 = bf16[16,16,80,32]{2,3,0,1:T(8,128)(2,1)S(1)} copy(bf16[16,16,80,32]{3,0,2,1:T(8,128)(2,1)} %bitcast.48) | data formatting | bytes 2621440 | tf_op jit(solution)/shard_map/all_to_all | solution.py:29
  84.4 1.6 %copy.18 = bf16[256,80,32]{0,1,2:T(8,128)(2,1)S(1)} copy(bf16[256,80,32]{1,2,0:T(8,128)(2,1)S(1)} %bitcast.51) | data formatting | bytes 2621440 | tf_op jit(solution)/shard_map/while | solution.py:22
  86.0 32.3 %while.10 = (s32[]{:T(128)}, bf16[4,8,80,128]{3,2,1,0:T(8,128)(2,1)}, bf16[4,256,8,32]{1,3,2,0:T(8,128)(2,1)}, bf16[256,80,32]{0,1,2:T(8,128)(2,1)S(1)}, bf16[10...) while((s32[]{:T(128)}, bf16[4,8,80,128]{3,2,1,0:T(8,128)(2,1)}, bf16[4,256,8,32]{1,3,2,0:T(8,128)(2,1)}, ...), condition=%wide.region_1.2_spmd, body=%wide.region_0.1_spmd.sunk | while | flops 504791040 | bytes 20547204 | solution.py:22
  86.0 1.1 copy-done
  87.1 1.6 %fusion.18 = bf16[8,80,32,32]{1,2,3,0:T(8,128)(2,1)S(1)} fusion(bf16[256,80,32]{0,1,2:T(8,128)(2,1)S(1)} %get-tuple-element.116, bf16[4,256,8,32]{1,3,2,0:T(8,128)(2,1)} %get-tuple-element.115, s32[]{:T(128)} %get-tuple-element.106), kind=kOutput, calls=%fused_computation.1.clone.1 | convolution fusion | flops 336855040 | bytes 2753024 | tf_op jit(solution)/shard_map/while/body/eval_jaxpr/sic,sje->ijce/dot_general | solution.py:11
  88.7 1.4 %copy.23 = bf16[8,80,32,32]{1,0,3,2:T(8,128)(2,1)S(1)} copy(bf16[8,80,32,32]{1,2,3,0:T(8,128)(2,1)S(1)} %fusion.18) | data formatting | bytes 2621440 | tf_op jit(solution)/shard_map/while/body/eval_jaxpr/convert_element_type | solution.py:14
  90.1 1.7 %reshape.21 = bf16[640,1024]{0,1:T(8,128)(2,1)S(1)} reshape(bf16[8,80,32,32]{1,0,3,2:T(8,128)(2,1)S(1)} %copy.23) | data formatting | bytes 2621440 | tf_op jit(solution)/shard_map/while/body/eval_jaxpr/reshape | solution.py:14
  91.8 1.6 %fusion.19 = bf16[640,128]{1,0:T(8,128)(2,1)S(1)} fusion(bf16[640,1024]{0,1:T(8,128)(2,1)S(1)} %reshape.21, bf16[1024,128]{1,0:T(8,128)(2,1)} %get-tuple-element.117, f32[128]{0:T(128)S(1)} %get-tuple-element.118), kind=kOutput, calls=%fused_computation.4.clone.1 | convolution fusion | flops 167936000 | bytes 1737216 | tf_op jit(solution)/shard_map/while/body/eval_jaxpr/dot_general | solution.py:15
  93.4 0.7 constant_dynamic-update-slice_fusion.2
  94.1 1.1 copy-done
  95.2 1.6 %fusion.18 = bf16[8,80,32,32]{1,2,3,0:T(8,128)(2,1)S(1)} fusion(bf16[256,80,32]{0,1,2:T(8,128)(2,1)S(1)} %get-tuple-element.116, bf16[4,256,8,32]{1,3,2,0:T(8,128)(2,1)} %get-tuple-element.115, s32[]{:T(128)} %get-tuple-element.106), kind=kOutput, calls=%fused_computation.1.clone.1 | convolution fusion | flops 336855040 | bytes 2753024 | tf_op jit(solution)/shard_map/while/body/eval_jaxpr/sic,sje->ijce/dot_general | solution.py:11
  96.8 1.4 %copy.23 = bf16[8,80,32,32]{1,0,3,2:T(8,128)(2,1)S(1)} copy(bf16[8,80,32,32]{1,2,3,0:T(8,128)(2,1)S(1)} %fusion.18) | data formatting | bytes 2621440 | tf_op jit(solution)/shard_map/while/body/eval_jaxpr/convert_element_type | solution.py:14
  98.2 1.7 %reshape.21 = bf16[640,1024]{0,1:T(8,128)(2,1)S(1)} reshape(bf16[8,80,32,32]{1,0,3,2:T(8,128)(2,1)S(1)} %copy.23) | data formatting | bytes 2621440 | tf_op jit(solution)/shard_map/while/body/eval_jaxpr/reshape | solution.py:14
  99.9 1.6 %fusion.19 = bf16[640,128]{1,0:T(8,128)(2,1)S(1)} fusion(bf16[640,1024]{0,1:T(8,128)(2,1)S(1)} %reshape.21, bf16[1024,128]{1,0:T(8,128)(2,1)} %get-tuple-element.117, f32[128]{0:T(128)S(1)} %get-tuple-element.118), kind=kOutput, calls=%fused_computation.4.clone.1 | convolution fusion | flops 167936000 | bytes 1737216 | tf_op jit(solution)/shard_map/while/body/eval_jaxpr/dot_general | solution.py:15
  102.2 1.1 copy-done
  103.2 1.6 %fusion.18 = bf16[8,80,32,32]{1,2,3,0:T(8,128)(2,1)S(1)} fusion(bf16[256,80,32]{0,1,2:T(8,128)(2,1)S(1)} %get-tuple-element.116, bf16[4,256,8,32]{1,3,2,0:T(8,128)(2,1)} %get-tuple-element.115, s32[]{:T(128)} %get-tuple-element.106), kind=kOutput, calls=%fused_computation.1.clone.1 | convolution fusion | flops 336855040 | bytes 2753024 | tf_op jit(solution)/shard_map/while/body/eval_jaxpr/sic,sje->ijce/dot_general | solution.py:11
  104.9 1.4 %copy.23 = bf16[8,80,32,32]{1,0,3,2:T(8,128)(2,1)S(1)} copy(bf16[8,80,32,32]{1,2,3,0:T(8,128)(2,1)S(1)} %fusion.18) | data formatting | bytes 2621440 | tf_op jit(solution)/shard_map/while/body/eval_jaxpr/convert_element_type | solution.py:14
  106.2 1.7 %reshape.21 = bf16[640,1024]{0,1:T(8,128)(2,1)S(1)} reshape(bf16[8,80,32,32]{1,0,3,2:T(8,128)(2,1)S(1)} %copy.23) | data formatting | bytes 2621440 | tf_op jit(solution)/shard_map/while/body/eval_jaxpr/reshape | solution.py:14
  108.0 1.6 %fusion.19 = bf16[640,128]{1,0:T(8,128)(2,1)S(1)} fusion(bf16[640,1024]{0,1:T(8,128)(2,1)S(1)} %reshape.21, bf16[1024,128]{1,0:T(8,128)(2,1)} %get-tuple-element.117, f32[128]{0:T(128)S(1)} %get-tuple-element.118), kind=kOutput, calls=%fused_computation.4.clone.1 | convolution fusion | flops 167936000 | bytes 1737216 | tf_op jit(solution)/shard_map/while/body/eval_jaxpr/dot_general | solution.py:15
  110.2 1.1 copy-done
  111.3 1.6 %fusion.18 = bf16[8,80,32,32]{1,2,3,0:T(8,128)(2,1)S(1)} fusion(bf16[256,80,32]{0,1,2:T(8,128)(2,1)S(1)} %get-tuple-element.116, bf16[4,256,8,32]{1,3,2,0:T(8,128)(2,1)} %get-tuple-element.115, s32[]{:T(128)} %get-tuple-element.106), kind=kOutput, calls=%fused_computation.1.clone.1 | convolution fusion | flops 336855040 | bytes 2753024 | tf_op jit(solution)/shard_map/while/body/eval_jaxpr/sic,sje->ijce/dot_general | solution.py:11
  113.0 1.4 %copy.23 = bf16[8,80,32,32]{1,0,3,2:T(8,128)(2,1)S(1)} copy(bf16[8,80,32,32]{1,2,3,0:T(8,128)(2,1)S(1)} %fusion.18) | data formatting | bytes 2621440 | tf_op jit(solution)/shard_map/while/body/eval_jaxpr/convert_element_type | solution.py:14
  114.3 1.7 %reshape.21 = bf16[640,1024]{0,1:T(8,128)(2,1)S(1)} reshape(bf16[8,80,32,32]{1,0,3,2:T(8,128)(2,1)S(1)} %copy.23) | data formatting | bytes 2621440 | tf_op jit(solution)/shard_map/while/body/eval_jaxpr/reshape | solution.py:14
  116.0 1.6 %fusion.19 = bf16[640,128]{1,0:T(8,128)(2,1)S(1)} fusion(bf16[640,1024]{0,1:T(8,128)(2,1)S(1)} %reshape.21, bf16[1024,128]{1,0:T(8,128)(2,1)} %get-tuple-element.117, f32[128]{0:T(128)S(1)} %get-tuple-element.118), kind=kOutput, calls=%fused_computation.4.clone.1 | convolution fusion | flops 167936000 | bytes 1737216 | tf_op jit(solution)/shard_map/while/body/eval_jaxpr/dot_general | solution.py:15
  (23 shorter events, 2.3 us)
Async XLA Ops:
  1.7 21.8 %all-to-all-start = ((bf16[16,2,512]{2,1,0:T(2,128)(2,1)}), bf16[16,2,512]{2,1,0:T(2,128)(2,1)S(1)}, u32[]{:S(2)}, u32[]{:S(2)}) async-start(bf16[16,2,512]{2,1,0:T(2,128)(2,1)} %reshape.16), calls=%async_computation | async-start | bytes 65536 | tf_op jit(solution)/shard_map/all_to_all | solution.py:28
  23.5 50.1 %all-to-all-start.1 = ((bf16[16,2,20480]{2,1,0:T(2,128)(2,1)}), bf16[16,2,20480]{2,1,0:T(2,128)(2,1)S(1)}, u32[]{:S(2)}, u32[]{:S(2)}) async-start(bf16[16,2,20480]{2,1,0:T(2,128)(2,1)} %reshape.18), calls=%async_computation.1 | async-start | bytes 2621440 | tf_op jit(solution)/shard_map/all_to_all | solution.py:29
  84.4 1.6 %copy-start.2 = (f32[128]{0:T(128)S(1)}, f32[128]{0:T(128)}, u32[]{:S(2)}) copy-start(f32[128]{0:T(128)} %param.9) | copy-start | bytes 1540
  86.0 1.1 copy-start
  91.8 2.3 %copy-start.1 = (bf16[256,80,32]{0,1,2:T(8,128)(2,1)S(1)}, bf16[256,80,32]{0,1,2:T(8,128)(2,1)}, u32[]{:S(2)}) copy-start(bf16[256,80,32]{0,1,2:T(8,128)(2,1)} %copy-done) | copy-start | bytes 3932164 | tf_op jit(solution)/shard_map/while
  94.1 1.1 copy-start
  99.9 2.3 %copy-start.1 = (bf16[256,80,32]{0,1,2:T(8,128)(2,1)S(1)}, bf16[256,80,32]{0,1,2:T(8,128)(2,1)}, u32[]{:S(2)}) copy-start(bf16[256,80,32]{0,1,2:T(8,128)(2,1)} %copy-done) | copy-start | bytes 3932164 | tf_op jit(solution)/shard_map/while
  102.2 1.1 copy-start
  107.9 2.3 %copy-start.1 = (bf16[256,80,32]{0,1,2:T(8,128)(2,1)S(1)}, bf16[256,80,32]{0,1,2:T(8,128)(2,1)}, u32[]{:S(2)}) copy-start(bf16[256,80,32]{0,1,2:T(8,128)(2,1)} %copy-done) | copy-start | bytes 3932164 | tf_op jit(solution)/shard_map/while
  110.2 1.1 copy-start
  116.0 2.3 %copy-start.1 = (bf16[256,80,32]{0,1,2:T(8,128)(2,1)S(1)}, bf16[256,80,32]{0,1,2:T(8,128)(2,1)}, u32[]{:S(2)}) copy-start(bf16[256,80,32]{0,1,2:T(8,128)(2,1)} %copy-done) | copy-start | bytes 3932164 | tf_op jit(solution)/shard_map/while
where the time goes:
time: 119 us; the launch traced here: 118 us
  local copies, waits for them, and re-layouts  48.7 us (41%)
  blocking collectives  43.8 us (37%)
  matrix products  12.9 us (11%)
  starting transfers between devices  12.6 us (11%)
    all_gather x1, blocking collectives, on_device(): lax.all_gather(left_part, 'col', axis=1, tiled=True)  43.8 us
    unnamed x8, local copies, waits for them, and re-layouts  21.1 us
    reshape x4, local copies, waits for them, and re-layouts, tile_update(): flat = outer.astype(jnp.bfloat16).reshape(count * columns, width * width)  6.79 us
    all_to_all x1, local copies, waits for them, and re-layouts, on_device(): lax.all_to_all(right, 'col', split_axis=1, concat_axis=0, tiled=True)  6.76 us
    all_to_all x1, starting transfers between devices, on_device(): lax.all_to_all(left, 'col', split_axis=1, concat_axis=0, tiled=True)  6.58 us
    dot_general x4, matrix products, tile_update(): jnp.einsum('sic,sje->ijce', left_rows, right_cols, preferred_element_type...  6.53 us
    dot_general x4, matrix products, tile_update(): jnp.dot(flat, out_weight, preferred_element_type=jnp.float32) + out_bias  6.39 us
    all_to_all x1, starting transfers between devices, on_device(): lax.all_to_all(right, 'col', split_axis=1, concat_axis=0, tiled=True)  6.02 us
  transfers between devices with their start and end apart: 2, of which 0 were waited for; matrix products, arithmetic and copies ran while one was open for 13% of the time, Pallas kernels for 0%

commit v1 on v0

--- a/solution.py
+++ b/solution.py
@@ -2,6 +2,18 @@
 import jax.numpy as jnp
 from jax import lax
 from jax.sharding import PartitionSpec as P
+
+
+def exchange_directly(x, axis, split, join):
+    ways, here = (lax.axis_size(axis), lax.axis_index(axis))
+    width = x.shape[split] // ways
+    turned = jnp.roll(x, -here * width, axis=split)
+    got = [lax.slice_in_dim(turned, 0, width, axis=split)]
+    for far in range(1, ways):
+        sent = lax.slice_in_dim(turned, far * width, (far + 1) * width, axis=split)
+        got.append(lax.ppermute(sent, axis, [(d, (d + far) % ways) for d in range(ways)]))
+    line = jnp.concatenate(got[::-1], axis=join)
+    return jnp.roll(line, (here + 1) * got[0].shape[join], axis=join)
 
 
 def tile_update(left_rows, right_cols, out_weight, out_bias):
@@ -26,7 +38,7 @@
 def on_device(left, right, out_weight, out_bias):
     left_part, right_cols = (
         lax.all_to_all(left, "col", split_axis=1, concat_axis=0, tiled=True),
-        lax.all_to_all(right, "col", split_axis=1, concat_axis=0, tiled=True),
+        exchange_directly(right, "col", 1, 0),
     )
     return rows_update(
         lax.all_gather(left_part, "col", axis=1, tiled=True), right_cols, out_weight, out_bias

time: 119 us -> 126 us (1.059)
  the two profiles are of different devices: /device:TPU:9 before, /device:TPU:0 now
where the time goes in v1:
time: 126 us; the launch traced here: 125 us
  blocking collectives  31.1 us (25%)
  starting transfers between devices  30.1 us (24%)
  waiting for transfers between devices  24.8 us (20%)
  local copies, waits for them, and re-layouts  22 us (17%)
  matrix products  14.5 us (12%)
  other arithmetic  2.52 us (2%)
    all_gather x1, blocking collectives, on_device(): lax.all_gather(left_part, 'col', axis=1, tiled=True)  31.1 us
    ppermute x15, waiting for transfers between devices, exchange_directly(): lax.ppermute(sent, axis, [(d, (d + far) % ways) for d in range(ways)])  24.8 us
    ppermute x15, starting transfers between devices, exchange_directly(): lax.ppermute(sent, axis, [(d, (d + far) % ways) for d in range(ways)])  22.7 us
    dot_general x4, matrix products, tile_update(): jnp.einsum('sic,sje->ijce', left_rows, right_cols, preferred_element_type...  8.49 us
    all_to_all x1, starting transfers between devices, on_device(): lax.all_to_all(left, 'col', split_axis=1, concat_axis=0, tiled=True)  7.41 us
    reshape x4, local copies, waits for them, and re-layouts, tile_update(): flat = outer.astype(jnp.bfloat16).reshape(count * columns, width * width)  6.79 us
    dot_general x4, matrix products, tile_update(): jnp.dot(flat, out_weight, preferred_element_type=jnp.float32) + out_bias  5.98 us
    convert_element_type x4, local copies, waits for them, and re-layouts, tile_update(): flat = outer.astype(jnp.bfloat16).reshape(count * columns, width * width)  5.42 us
  transfers between devices with their start and end apart: 16, of which 7 were waited for; matrix products, arithmetic and copies ran while one was open for 4% of the time, Pallas kernels for 0%

profile of v1, /device:TPU:0, one launch (start us, length us, event | category | flops | bytes accessed | tf_op | source)
XLA Modules:
  0.0 125.4 jit_solution(15973454242592859153)
XLA Ops:
  0.0 1.0 copy.20
  1.7 7.4 %all-to-all-start = ((bf16[16,2,512]{2,1,0:T(2,128)(2,1)}), bf16[16,2,512]{2,1,0:T(2,128)(2,1)S(1)}, u32[]{:S(2)}, u32[]{:S(2)}) async-start(bf16[16,2,512]{2,1,0:T(2,128)(2,1)} %reshape.16), calls=%async_computation | async-start | bytes 65536 | tf_op jit(solution)/shard_map/all_to_all | solution.py:40
  9.2 2.5 %fusion.6 = bf16[16,1280,32]{1,2,0:T(8,128)(2,1)S(1)} fusion(s32[]{:T(128)S(6)} %select_n.24, bf16[16,1280,32]{1,2,0:T(8,128)(2,1)} %param.7), kind=kLoop, calls=%fused_computation.11 | loop fusion | flops 2621440 | bytes 2621444 | tf_op jit(solution)/shard_map/jit(_roll_dynamic)/concatenate | solution.py:10
  11.7 1.4 %fusion.7 = (bf16[16,80,32]{1,2,0:T(8,128)(2,1)S(1)}, bf16[16,80,32]{1,2,0:T(8,128)(2,1)S(1)}, bf16[16,80,32]{1,2,0:T(8,128)(2,1)S(1)}, bf16[16,80,32]{1,2,0:T(8...) fusion(bf16[16,1280,32]{1,2,0:T(8,128)(2,1)S(1)} %fusion.6), kind=kLoop, calls=%fused_computation.45 | loop fusion | bytes 2457600 | tf_op jit(solution)/shard_map/slice | solution.py:13
  13.1 4.4 %collective-permute-start = (bf16[16,80,32]{1,2,0:T(8,128)(2,1)}, bf16[16,80,32]{1,2,0:T(8,128)(2,1)S(1)}, u32[]{:S(2)}, u32[]{:S(2)}) collective-permute-start(bf16[16,80,32]{1,2,0:T(8,128)(2,1)} %get-tuple-element.70), channel_id=1, source_target_pairs={{0,15},{1,0},{2,1},{3,2},{4,3},{5,4},{6,5},{7,6},{8,7},{9,8},{10,9... | collective-permute-start | bytes 245768 | tf_op jit(solution)/shard_map/ppermute | solution.py:14
  19.2 31.1 %all_gather.3 = bf16[256,32,32]{0,2,1:T(8,128)(2,1)} all-gather(bf16[256,2,32]{0,2,1:T(8,128)(2,1)S(1)} %copy.16), channel_id=1, replica_groups=mesh['groups'=2,'col'=16] {'col'}, dimensions={1}, use_global_device_ids=true | all-gather | bytes 557056 | tf_op jit(solution)/shard_map/all_gather | solution.py:44
  50.4 2.9 %collective-permute-start.7 = (bf16[16,80,32]{1,2,0:T(8,128)(2,1)S(1)}, bf16[16,80,32]{1,2,0:T(8,128)(2,1)S(1)}, u32[]{:S(2)}, u32[]{:S(2)}) collective-permute-start(bf16[16,80,32]{1,2,0:T(8,128)(2,1)S(1)} %get-tuple-element.63), channel_id=1, source_target_pairs={{0,8},{1,9},{2,10},{3,11},{4,12},{5,13},{6,14},{7,15},{8,0},{9,1},... | collective-permute-start | bytes 245768 | tf_op jit(solution)/shard_map/ppermute | solution.py:14
  53.5 3.6 %collective-permute-start.9 = (bf16[16,80,32]{1,2,0:T(8,128)(2,1)S(1)}, bf16[16,80,32]{1,2,0:T(8,128)(2,1)S(1)}, u32[]{:S(2)}, u32[]{:S(2)}) collective-permute-start(bf16[16,80,32]{1,2,0:T(8,128)(2,1)S(1)} %get-tuple-element.61), channel_id=1, source_target_pairs={{0,6},{1,7},{2,8},{3,9},{4,10},{5,11},{6,12},{7,13},{8,14},{9,15},... | collective-permute-start | bytes 245768 | tf_op jit(solution)/shard_map/ppermute | solution.py:14
  58.7 10.2 %collective-permute-start.11 = (bf16[16,80,32]{1,2,0:T(8,128)(2,1)S(1)}, bf16[16,80,32]{1,2,0:T(8,128)(2,1)S(1)}, u32[]{:S(2)}, u32[]{:S(2)}) collective-permute-start(bf16[16,80,32]{1,2,0:T(8,128)(2,1)S(1)} %get-tuple-element.59), channel_id=1, source_target_pairs={{0,4},{1,5},{2,6},{3,7},{4,8},{5,9},{6,10},{7,11},{8,12},{9,13},{1... | collective-permute-start | bytes 245768 | tf_op jit(solution)/shard_map/ppermute | solution.py:14
  68.9 6.9 %collective-permute-done.7 = bf16[16,80,32]{1,2,0:T(8,128)(2,1)S(1)} collective-permute-done((bf16[16,80,32]{1,2,0:T(8,128)(2,1)S(1)}, bf16[16,80,32]{1,2,0:T(8,128)(2,1)S(1)}, u32[]{:S(2)}, u32[]{:S(2)}) %collective-permute-start.7) | collective-permute-done | bytes 81952 | tf_op jit(solution)/shard_map/ppermute | solution.py:14
  75.8 3.6 %collective-permute-done.8 = bf16[16,80,32]{1,2,0:T(8,128)(2,1)S(1)} collective-permute-done((bf16[16,80,32]{1,2,0:T(8,128)(2,1)S(1)}, bf16[16,80,32]{1,2,0:T(8,128)(2,1)S(1)}, u32[]{:S(2)}, u32[]{:S(2)}) %collective-permute-start.8) | collective-permute-done | bytes 81952 | tf_op jit(solution)/shard_map/ppermute | solution.py:14
  79.4 5.8 %collective-permute-done.9 = bf16[16,80,32]{1,2,0:T(8,128)(2,1)S(1)} collective-permute-done((bf16[16,80,32]{1,2,0:T(8,128)(2,1)S(1)}, bf16[16,80,32]{1,2,0:T(8,128)(2,1)S(1)}, u32[]{:S(2)}, u32[]{:S(2)}) %collective-permute-start.9) | collective-permute-done | bytes 81952 | tf_op jit(solution)/shard_map/ppermute | solution.py:14
  85.3 2.2 %collective-permute-done.10 = bf16[16,80,32]{1,2,0:T(8,128)(2,1)S(1)} collective-permute-done((bf16[16,80,32]{1,2,0:T(8,128)(2,1)S(1)}, bf16[16,80,32]{1,2,0:T(8,128)(2,1)S(1)}, u32[]{:S(2)}, u32[]{:S(2)}) %collective-permute-start.10) | collective-permute-done | bytes 81952 | tf_op jit(solution)/shard_map/ppermute | solution.py:14
  87.6 4.8 %collective-permute-done.14 = bf16[16,80,32]{1,2,0:T(8,128)(2,1)S(1)} collective-permute-done((bf16[16,80,32]{1,2,0:T(8,128)(2,1)S(1)}, bf16[16,80,32]{1,2,0:T(8,128)(2,1)S(1)}, u32[]{:S(2)}, u32[]{:S(2)}) %collective-permute-start.14) | collective-permute-done | bytes 81952 | tf_op jit(solution)/shard_map/ppermute | solution.py:14
  93.2 2.6 %copy.17 = bf16[256,80,32]{0,1,2:T(8,128)(2,1)} copy(bf16[256,80,32]{1,2,0:T(8,128)(2,1)S(1)} %constant_dynamic-slice_fusion) | data formatting | bytes 2621440 | tf_op jit(solution)/shard_map/while | solution.py:34
  95.9 29.5 %while.10 = (s32[]{:T(128)}, bf16[4,8,80,128]{3,2,1,0:T(8,128)(2,1)}, bf16[4,256,8,32]{1,3,2,0:T(8,128)(2,1)}, bf16[256,80,32]{0,1,2:T(8,128)(2,1)}, bf16[1024,1...) while((s32[]{:T(128)}, bf16[4,8,80,128]{3,2,1,0:T(8,128)(2,1)}, bf16[4,256,8,32]{1,3,2,0:T(8,128)(2,1)}, ...), condition=%wide.region_1.2_spmd, body=%wide.region_0.1_spmd.sunk | while | flops 504791040 | bytes 10061389 | solution.py:34
  95.9 2.1 %fusion.20 = bf16[8,80,32,32]{1,2,3,0:T(8,128)(2,1)S(1)} fusion(bf16[256,80,32]{0,1,2:T(8,128)(2,1)} %get-tuple-element.125, bf16[4,256,8,32]{1,3,2,0:T(8,128)(2,1)} %get-tuple-element.124, s32[]{:T(128)} %get-tuple-element.115), kind=kOutput, calls=%fused_computation.1.clone.1 | convolution fusion | flops 336855040 | bytes 2753024 | tf_op jit(solution)/shard_map/while/body/eval_jaxpr/sic,sje->ijce/dot_general | solution.py:23
  98.0 1.4 %copy.22 = bf16[8,80,32,32]{1,0,3,2:T(8,128)(2,1)S(1)} copy(bf16[8,80,32,32]{1,2,3,0:T(8,128)(2,1)S(1)} %fusion.20) | data formatting | bytes 2621440 | tf_op jit(solution)/shard_map/while/body/eval_jaxpr/convert_element_type | solution.py:26
  99.4 1.7 %reshape.19 = bf16[640,1024]{0,1:T(8,128)(2,1)S(1)} reshape(bf16[8,80,32,32]{1,0,3,2:T(8,128)(2,1)S(1)} %copy.22) | data formatting | bytes 2621440 | tf_op jit(solution)/shard_map/while/body/eval_jaxpr/reshape | solution.py:26
  101.1 1.5 %fusion.21 = bf16[640,128]{1,0:T(8,128)(2,1)S(1)} fusion(bf16[640,1024]{0,1:T(8,128)(2,1)S(1)} %reshape.19, bf16[1024,128]{1,0:T(8,128)(2,1)} %get-tuple-element.126, f32[128]{0:T(128)S(1)} %get-tuple-element.127), kind=kOutput, calls=%fused_computation.4.clone.1 | convolution fusion | flops 167936000 | bytes 1737216 | tf_op jit(solution)/shard_map/while/body/eval_jaxpr/dot_general | solution.py:27
  103.3 2.1 %fusion.20 = bf16[8,80,32,32]{1,2,3,0:T(8,128)(2,1)S(1)} fusion(bf16[256,80,32]{0,1,2:T(8,128)(2,1)} %get-tuple-element.125, bf16[4,256,8,32]{1,3,2,0:T(8,128)(2,1)} %get-tuple-element.124, s32[]{:T(128)} %get-tuple-element.115), kind=kOutput, calls=%fused_computation.1.clone.1 | convolution fusion | flops 336855040 | bytes 2753024 | tf_op jit(solution)/shard_map/while/body/eval_jaxpr/sic,sje->ijce/dot_general | solution.py:23
  105.4 1.4 %copy.22 = bf16[8,80,32,32]{1,0,3,2:T(8,128)(2,1)S(1)} copy(bf16[8,80,32,32]{1,2,3,0:T(8,128)(2,1)S(1)} %fusion.20) | data formatting | bytes 2621440 | tf_op jit(solution)/shard_map/while/body/eval_jaxpr/convert_element_type | solution.py:26
  106.8 1.7 %reshape.19 = bf16[640,1024]{0,1:T(8,128)(2,1)S(1)} reshape(bf16[8,80,32,32]{1,0,3,2:T(8,128)(2,1)S(1)} %copy.22) | data formatting | bytes 2621440 | tf_op jit(solution)/shard_map/while/body/eval_jaxpr/reshape | solution.py:26
  108.5 1.5 %fusion.21 = bf16[640,128]{1,0:T(8,128)(2,1)S(1)} fusion(bf16[640,1024]{0,1:T(8,128)(2,1)S(1)} %reshape.19, bf16[1024,128]{1,0:T(8,128)(2,1)} %get-tuple-element.126, f32[128]{0:T(128)S(1)} %get-tuple-element.127), kind=kOutput, calls=%fused_computation.4.clone.1 | convolution fusion | flops 167936000 | bytes 1737216 | tf_op jit(solution)/shard_map/while/body/eval_jaxpr/dot_general | solution.py:27
  110.7 2.1 %fusion.20 = bf16[8,80,32,32]{1,2,3,0:T(8,128)(2,1)S(1)} fusion(bf16[256,80,32]{0,1,2:T(8,128)(2,1)} %get-tuple-element.125, bf16[4,256,8,32]{1,3,2,0:T(8,128)(2,1)} %get-tuple-element.124, s32[]{:T(128)} %get-tuple-element.115), kind=kOutput, calls=%fused_computation.1.clone.1 | convolution fusion | flops 336855040 | bytes 2753024 | tf_op jit(solution)/shard_map/while/body/eval_jaxpr/sic,sje->ijce/dot_general | solution.py:23
  112.8 1.4 %copy.22 = bf16[8,80,32,32]{1,0,3,2:T(8,128)(2,1)S(1)} copy(bf16[8,80,32,32]{1,2,3,0:T(8,128)(2,1)S(1)} %fusion.20) | data formatting | bytes 2621440 | tf_op jit(solution)/shard_map/while/body/eval_jaxpr/convert_element_type | solution.py:26
  114.1 1.7 %reshape.19 = bf16[640,1024]{0,1:T(8,128)(2,1)S(1)} reshape(bf16[8,80,32,32]{1,0,3,2:T(8,128)(2,1)S(1)} %copy.22) | data formatting | bytes 2621440 | tf_op jit(solution)/shard_map/while/body/eval_jaxpr/reshape | solution.py:26
  115.8 1.5 %fusion.21 = bf16[640,128]{1,0:T(8,128)(2,1)S(1)} fusion(bf16[640,1024]{0,1:T(8,128)(2,1)S(1)} %reshape.19, bf16[1024,128]{1,0:T(8,128)(2,1)} %get-tuple-element.126, f32[128]{0:T(128)S(1)} %get-tuple-element.127), kind=kOutput, calls=%fused_computation.4.clone.1 | convolution fusion | flops 167936000 | bytes 1737216 | tf_op jit(solution)/shard_map/while/body/eval_jaxpr/dot_general | solution.py:27
  118.0 2.1 %fusion.20 = bf16[8,80,32,32]{1,2,3,0:T(8,128)(2,1)S(1)} fusion(bf16[256,80,32]{0,1,2:T(8,128)(2,1)} %get-tuple-element.125, bf16[4,256,8,32]{1,3,2,0:T(8,128)(2,1)} %get-tuple-element.124, s32[]{:T(128)} %get-tuple-element.115), kind=kOutput, calls=%fused_computation.1.clone.1 | convolution fusion | flops 336855040 | bytes 2753024 | tf_op jit(solution)/shard_map/while/body/eval_jaxpr/sic,sje->ijce/dot_general | solution.py:23
  120.2 1.4 %copy.22 = bf16[8,80,32,32]{1,0,3,2:T(8,128)(2,1)S(1)} copy(bf16[8,80,32,32]{1,2,3,0:T(8,128)(2,1)S(1)} %fusion.20) | data formatting | bytes 2621440 | tf_op jit(solution)/shard_map/while/body/eval_jaxpr/convert_element_type | solution.py:26
  121.5 1.7 %reshape.19 = bf16[640,1024]{0,1:T(8,128)(2,1)S(1)} reshape(bf16[8,80,32,32]{1,0,3,2:T(8,128)(2,1)S(1)} %copy.22) | data formatting | bytes 2621440 | tf_op jit(solution)/shard_map/while/body/eval_jaxpr/reshape | solution.py:26
  123.2 1.5 %fusion.21 = bf16[640,128]{1,0:T(8,128)(2,1)S(1)} fusion(bf16[640,1024]{0,1:T(8,128)(2,1)S(1)} %reshape.19, bf16[1024,128]{1,0:T(8,128)(2,1)} %get-tuple-element.126, f32[128]{0:T(128)S(1)} %get-tuple-element.127), kind=kOutput, calls=%fused_computation.4.clone.1 | convolution fusion | flops 167936000 | bytes 1737216 | tf_op jit(solution)/shard_map/while/body/eval_jaxpr/dot_general | solution.py:27
  (66 shorter events, 7.9 us)
Async XLA Ops:
  1.7 17.2 %all-to-all-start = ((bf16[16,2,512]{2,1,0:T(2,128)(2,1)}), bf16[16,2,512]{2,1,0:T(2,128)(2,1)S(1)}, u32[]{:S(2)}, u32[]{:S(2)}) async-start(bf16[16,2,512]{2,1,0:T(2,128)(2,1)} %reshape.16), calls=%async_computation | async-start | bytes 65536 | tf_op jit(solution)/shard_map/all_to_all | solution.py:40
  13.1 37.2 %collective-permute-start = (bf16[16,80,32]{1,2,0:T(8,128)(2,1)}, bf16[16,80,32]{1,2,0:T(8,128)(2,1)S(1)}, u32[]{:S(2)}, u32[]{:S(2)}) collective-permute-start(bf16[16,80,32]{1,2,0:T(8,128)(2,1)} %get-tuple-element.70), channel_id=1, source_target_pairs={{0,15},{1,0},{2,1},{3,2},{4,3},{5,4},{6,5},{7,6},{8,7},{9,8},{10,9... | collective-permute-start | bytes 245768 | tf_op jit(solution)/shard_map/ppermute | solution.py:14
  17.5 32.8 %collective-permute-start.1 = (bf16[16,80,32]{1,2,0:T(8,128)(2,1)}, bf16[16,80,32]{1,2,0:T(8,128)(2,1)S(1)}, u32[]{:S(2)}, u32[]{:S(2)}) collective-permute-start(bf16[16,80,32]{1,2,0:T(8,128)(2,1)} %get-tuple-element.69), channel_id=1, source_target_pairs={{0,14},{1,15},{2,0},{3,1},{4,2},{5,3},{6,4},{7,5},{8,6},{9,7},{10,... | collective-permute-start | bytes 245768 | tf_op jit(solution)/shard_map/ppermute | solution.py:14
  18.0 32.4 %collective-permute-start.2 = (bf16[16,80,32]{1,2,0:T(8,128)(2,1)}, bf16[16,80,32]{1,2,0:T(8,128)(2,1)S(1)}, u32[]{:S(2)}, u32[]{:S(2)}) collective-permute-start(bf16[16,80,32]{1,2,0:T(8,128)(2,1)} %get-tuple-element.68), channel_id=1, source_target_pairs={{0,13},{1,14},{2,15},{3,0},{4,1},{5,2},{6,3},{7,4},{8,5},{9,6},{10... | collective-permute-start | bytes 245768 | tf_op jit(solution)/shard_map/ppermute | solution.py:14
  18.1 35.2 %collective-permute-start.3 = (bf16[16,80,32]{1,2,0:T(8,128)(2,1)}, bf16[16,80,32]{1,2,0:T(8,128)(2,1)S(1)}, u32[]{:S(2)}, u32[]{:S(2)}) collective-permute-start(bf16[16,80,32]{1,2,0:T(8,128)(2,1)} %get-tuple-element.67), channel_id=1, source_target_pairs={{0,12},{1,13},{2,14},{3,15},{4,0},{5,1},{6,2},{7,3},{8,4},{9,5},{1... | collective-permute-start | bytes 245768 | tf_op jit(solution)/shard_map/ppermute | solution.py:14
  18.7 34.7 %collective-permute-start.4 = (bf16[16,80,32]{1,2,0:T(8,128)(2,1)}, bf16[16,80,32]{1,2,0:T(8,128)(2,1)S(1)}, u32[]{:S(2)}, u32[]{:S(2)}) collective-permute-start(bf16[16,80,32]{1,2,0:T(8,128)(2,1)} %get-tuple-element.66), channel_id=1, source_target_pairs={{0,11},{1,12},{2,13},{3,14},{4,15},{5,0},{6,1},{7,2},{8,3},{9,4},{... | collective-permute-start | bytes 245768 | tf_op jit(solution)/shard_map/ppermute | solution.py:14
  50.3 7.7 %collective-permute-start.5 = (bf16[16,80,32]{1,2,0:T(8,128)(2,1)S(1)}, bf16[16,80,32]{1,2,0:T(8,128)(2,1)S(1)}, u32[]{:S(2)}, u32[]{:S(2)}) collective-permute-start(bf16[16,80,32]{1,2,0:T(8,128)(2,1)S(1)} %get-tuple-element.65), channel_id=1, source_target_pairs={{0,10},{1,11},{2,12},{3,13},{4,14},{5,15},{6,0},{7,1},{8,2},{9,3},... | collective-permute-start | bytes 245768 | tf_op jit(solution)/shard_map/ppermute | solution.py:14
  50.3 8.4 %collective-permute-start.6 = (bf16[16,80,32]{1,2,0:T(8,128)(2,1)S(1)}, bf16[16,80,32]{1,2,0:T(8,128)(2,1)S(1)}, u32[]{:S(2)}, u32[]{:S(2)}) collective-permute-start(bf16[16,80,32]{1,2,0:T(8,128)(2,1)S(1)} %get-tuple-element.64), channel_id=1, source_target_pairs={{0,9},{1,10},{2,11},{3,12},{4,13},{5,14},{6,15},{7,0},{8,1},{9,2},... | collective-permute-start | bytes 245768 | tf_op jit(solution)/shard_map/ppermute | solution.py:14
  50.4 25.4 %collective-permute-start.7 = (bf16[16,80,32]{1,2,0:T(8,128)(2,1)S(1)}, bf16[16,80,32]{1,2,0:T(8,128)(2,1)S(1)}, u32[]{:S(2)}, u32[]{:S(2)}) collective-permute-start(bf16[16,80,32]{1,2,0:T(8,128)(2,1)S(1)} %get-tuple-element.63), channel_id=1, source_target_pairs={{0,8},{1,9},{2,10},{3,11},{4,12},{5,13},{6,14},{7,15},{8,0},{9,1},... | collective-permute-start | bytes 245768 | tf_op jit(solution)/shard_map/ppermute | solution.py:14
  53.4 26.0 %collective-permute-start.8 = (bf16[16,80,32]{1,2,0:T(8,128)(2,1)S(1)}, bf16[16,80,32]{1,2,0:T(8,128)(2,1)S(1)}, u32[]{:S(2)}, u32[]{:S(2)}) collective-permute-start(bf16[16,80,32]{1,2,0:T(8,128)(2,1)S(1)} %get-tuple-element.62), channel_id=1, source_target_pairs={{0,7},{1,8},{2,9},{3,10},{4,11},{5,12},{6,13},{7,14},{8,15},{9,0},... | collective-permute-start | bytes 245768 | tf_op jit(solution)/shard_map/ppermute | solution.py:14
  53.5 31.8 %collective-permute-start.9 = (bf16[16,80,32]{1,2,0:T(8,128)(2,1)S(1)}, bf16[16,80,32]{1,2,0:T(8,128)(2,1)S(1)}, u32[]{:S(2)}, u32[]{:S(2)}) collective-permute-start(bf16[16,80,32]{1,2,0:T(8,128)(2,1)S(1)} %get-tuple-element.61), channel_id=1, source_target_pairs={{0,6},{1,7},{2,8},{3,9},{4,10},{5,11},{6,12},{7,13},{8,14},{9,15},... | collective-permute-start | bytes 245768 | tf_op jit(solution)/shard_map/ppermute | solution.py:14
  57.9 29.5 %collective-permute-start.10 = (bf16[16,80,32]{1,2,0:T(8,128)(2,1)S(1)}, bf16[16,80,32]{1,2,0:T(8,128)(2,1)S(1)}, u32[]{:S(2)}, u32[]{:S(2)}) collective-permute-start(bf16[16,80,32]{1,2,0:T(8,128)(2,1)S(1)} %get-tuple-element.60), channel_id=1, source_target_pairs={{0,5},{1,6},{2,7},{3,8},{4,9},{5,10},{6,11},{7,12},{8,13},{9,14},{... | collective-permute-start | bytes 245768 | tf_op jit(solution)/shard_map/ppermute | solution.py:14
  58.7 28.7 %collective-permute-start.11 = (bf16[16,80,32]{1,2,0:T(8,128)(2,1)S(1)}, bf16[16,80,32]{1,2,0:T(8,128)(2,1)S(1)}, u32[]{:S(2)}, u32[]{:S(2)}) collective-permute-start(bf16[16,80,32]{1,2,0:T(8,128)(2,1)S(1)} %get-tuple-element.59), channel_id=1, source_target_pairs={{0,4},{1,5},{2,6},{3,7},{4,8},{5,9},{6,10},{7,11},{8,12},{9,13},{1... | collective-permute-start | bytes 245768 | tf_op jit(solution)/shard_map/ppermute | solution.py:14
  75.8 11.7 %collective-permute-start.12 = (bf16[16,80,32]{1,2,0:T(8,128)(2,1)S(1)}, bf16[16,80,32]{1,2,0:T(8,128)(2,1)S(1)}, u32[]{:S(2)}, u32[]{:S(2)}) collective-permute-start(bf16[16,80,32]{1,2,0:T(8,128)(2,1)S(1)} %get-tuple-element.58), channel_id=1, source_target_pairs={{0,3},{1,4},{2,5},{3,6},{4,7},{5,8},{6,9},{7,10},{8,11},{9,12},{10... | collective-permute-start | bytes 245768 | tf_op jit(solution)/shard_map/ppermute | solution.py:14
  79.4 8.1 %collective-permute-start.13 = (bf16[16,80,32]{1,2,0:T(8,128)(2,1)S(1)}, bf16[16,80,32]{1,2,0:T(8,128)(2,1)S(1)}, u32[]{:S(2)}, u32[]{:S(2)}) collective-permute-start(bf16[16,80,32]{1,2,0:T(8,128)(2,1)S(1)} %get-tuple-element.57), channel_id=1, source_target_pairs={{0,2},{1,3},{2,4},{3,5},{4,6},{5,7},{6,8},{7,9},{8,10},{9,11},{10,... | collective-permute-start | bytes 245768 | tf_op jit(solution)/shard_map/ppermute | solution.py:14
  85.2 7.1 %collective-permute-start.14 = (bf16[16,80,32]{1,2,0:T(8,128)(2,1)S(1)}, bf16[16,80,32]{1,2,0:T(8,128)(2,1)S(1)}, u32[]{:S(2)}, u32[]{:S(2)}) collective-permute-start(bf16[16,80,32]{1,2,0:T(8,128)(2,1)S(1)} %get-tuple-element.56), channel_id=1, source_target_pairs={{0,1},{1,2},{2,3},{3,4},{4,5},{5,6},{6,7},{7,8},{8,9},{9,10},{10,1... | collective-permute-start | bytes 245768 | tf_op jit(solution)/shard_map/ppermute | solution.py:14
  92.8 3.1 %copy-start = (f32[128]{0:T(128)S(1)}, f32[128]{0:T(128)}, u32[]{:S(2)}) copy-start(f32[128]{0:T(128)} %param.9) | copy-start | bytes 1540
